TPU v7x, 32 devices: a whole 2x2x4 slice. The times are simulated.
32 devices in a mesh: fsdp: 8 (over z, y), tp: 4 (over x, core).
Axes of the slice: x: 2, y: 2, z: 4, core: 2. Of those that a mesh axis runs over, the one named last changes fastest.
Arguments:
- tokens: bfloat16 [16384, 768], P(('fsdp', 'tp')), may hold values from -6 to 6
- pass_ids: int32 [16384], P(('fsdp', 'tp')), may hold values from 0 to 4
- prefix: int32 [8], P('fsdp'), may hold values from 0 to 2047
- cotangent: bfloat16 [16384, 768], P(('fsdp', 'tp')), may hold values from -6 to 6
- qkv_weight: bfloat16 [3, 768, 768], P(None, 'fsdp', 'tp'), may hold values from -0.21875 to 0.21875
- out_weight: bfloat16 [768, 768], P('tp', 'fsdp'), may hold values from -1.75 to 1.75
- fc1_weight: bfloat16 [768, 3072], P('fsdp', 'tp'), may hold values from -0.21875 to 0.21875
- fc2_weight: bfloat16 [3072, 768], P('tp', 'fsdp'), may hold values from -0.109375 to 0.109375
- ln1_gain: float32 [768], replicated, may hold values from 0.1 to 1.9
- ln1_bias: float32 [768], replicated, may hold values from -2 to 2
- qv_bias: float32 [2, 768], replicated, may hold values from -2 to 2
- out_bias: float32 [768], replicated, may hold values from -2 to 2
- ln2_gain: float32 [768], replicated, may hold values from 0.1 to 1.9
- ln2_bias: float32 [768], replicated, may hold values from -2 to 2
- fc1_bias: float32 [3072], replicated, may hold values from -3 to 3
- fc2_bias: float32 [768], replicated, may hold values from -2 to 2
- pass_table: float32 [5, 768], replicated, may hold values from -3 to 3
Outputs:
- activations: bfloat16 [16384, 768], P(('fsdp', 'tp'))
- input_grad: float32 [16384, 768], P(('fsdp', 'tp'))
- qkv_grad: float32 [3, 768, 768], P(None, 'fsdp', 'tp')
- out_grad: float32 [768, 768], P('tp', 'fsdp')
- fc1_grad: float32 [768, 3072], P('fsdp', 'tp')
- fc2_grad: float32 [3072, 768], P('tp', 'fsdp')
- ln1_gain_grad: float32 [768], replicated
- ln1_bias_grad: float32 [768], replicated
- qv_bias_grad: float32 [2, 768], replicated
- out_bias_grad: float32 [768], replicated
- ln2_gain_grad: float32 [768], replicated
- ln2_bias_grad: float32 [768], replicated
- fc1_bias_grad: float32 [3072], replicated
- fc2_bias_grad: float32 [768], replicated
- pass_table_grad: float32 [5, 768], replicated
All inputs are finite; a program needn't handle non-finite values.
Results may differ from a plain program's by a relative error of at most 0.009.
Values may be sent and summed in bfloat16 or wider, within the bound.
A program may use at most 128 MiB of HBM per device.

v0:
```python
from functools import partial
import jax
import jax.numpy as jnp
from jax import lax
from jax.sharding import PartitionSpec as P

HD = 64
NPASS = 5
QBLOCK = 512
HIGH = lax.Precision.HIGHEST
EPS = 1e-05
NEG_FILL = -1e30


def norm_forward(rows_in, gain, shift):
    center = rows_in - jnp.mean(rows_in, axis=-1, keepdims=True)
    scale_inv = lax.rsqrt(jnp.mean(center * center, axis=-1, keepdims=True) + EPS)
    unit_rows = center * scale_inv
    return (unit_rows * gain + shift, unit_rows, scale_inv)


def norm_backward(grad_out, unit_rows, scale_inv, gain):
    grad_unit = grad_out * gain
    first_mean = jnp.mean(grad_unit, axis=-1, keepdims=True)
    second_mean = jnp.mean(grad_unit * unit_rows, axis=-1, keepdims=True)
    grad_rows = scale_inv * (grad_unit - first_mean - unit_rows * second_mean)
    return (grad_rows, jnp.sum(grad_out * unit_rows, axis=0), jnp.sum(grad_out, axis=0))


def matmul_nt(left, right):
    return lax.dot_general(
        left, right, (((1,), (1,)), ((), ())), preferred_element_type=jnp.float32
    )


def matmul_tn(left, right):
    return lax.dot_general(
        left, right, (((0,), (0,)), ((), ())), preferred_element_type=jnp.float32
    )


def block_scores(query_block, keys_all, row_start, prefix_len, scale):
    raw = (
        jnp.einsum("qhe,khe->hqk", query_block, keys_all, preferred_element_type=jnp.float32)
        * scale
    )
    row_ids = row_start + jnp.arange(query_block.shape[0], dtype=jnp.int32)
    col_ids = jnp.arange(keys_all.shape[0], dtype=jnp.int32)
    allowed = (col_ids[None, :] <= row_ids[:, None]) | (col_ids[None, :] < prefix_len)
    return jnp.where(allowed[None], raw, NEG_FILL)


def attend_forward(queries, keys_all, values_all, prefix_len, scale):
    seq_len, heads_here, head_size = queries.shape
    block_count = seq_len // QBLOCK
    query_blocks = queries.reshape(block_count, QBLOCK, heads_here, head_size)
    block_starts = jnp.arange(block_count, dtype=jnp.int32) * QBLOCK

    def one_block(item):
        query_block, row_start = item
        masked = block_scores(query_block, keys_all, row_start, prefix_len, scale)
        peak = jnp.max(masked, axis=-1, keepdims=True)
        expo = jnp.exp(masked - peak)
        total_mass = jnp.sum(expo, axis=-1, keepdims=True)
        probs_low = (expo / total_mass).astype(jnp.bfloat16)
        out_block = jnp.einsum(
            "hqk,khe->qhe", probs_low, values_all, preferred_element_type=jnp.float32
        )
        return (out_block.astype(jnp.bfloat16), (peak + jnp.log(total_mass))[..., 0])

    outputs, log_mass = lax.map(one_block, (query_blocks, block_starts))
    return (outputs.reshape(seq_len, heads_here * head_size), log_mass)


def attend_backward(queries, keys_all, values_all, grad_mixed, log_mass, prefix_len, scale):
    seq_len, heads_here, head_size = queries.shape
    block_count = seq_len // QBLOCK
    query_blocks = queries.reshape(block_count, QBLOCK, heads_here, head_size)
    grad_blocks = grad_mixed.reshape(block_count, QBLOCK, heads_here, head_size)
    block_starts = jnp.arange(block_count, dtype=jnp.int32) * QBLOCK

    def one_block(carry, item):
        grad_keys, grad_values = carry
        query_block, grad_block, block_mass, row_start = item
        masked = block_scores(query_block, keys_all, row_start, prefix_len, scale)
        probs = jnp.exp(masked - block_mass[..., None])
        probs_low = probs.astype(jnp.bfloat16)
        grad_values = grad_values + jnp.einsum(
            "hqk,qhe->khe", probs_low, grad_block, preferred_element_type=jnp.float32
        )
        grad_probs = jnp.einsum(
            "qhe,khe->hqk", grad_block, values_all, preferred_element_type=jnp.float32
        )
        inner_sum = jnp.sum(probs * grad_probs, axis=-1, keepdims=True)
        grad_scores = (probs * (grad_probs - inner_sum)).astype(jnp.bfloat16)
        grad_query = (
            jnp.einsum("hqk,khe->qhe", grad_scores, keys_all, preferred_element_type=jnp.float32)
            * scale
        )
        grad_keys = (
            grad_keys
            + jnp.einsum(
                "hqk,qhe->khe", grad_scores, query_block, preferred_element_type=jnp.float32
            )
            * scale
        )
        return ((grad_keys, grad_values), grad_query)

    zero_state = jnp.zeros(keys_all.shape, jnp.float32)
    (grad_keys, grad_values), grad_queries = lax.scan(
        one_block, (zero_state, zero_state), (query_blocks, grad_blocks, log_mass, block_starts)
    )
    return (grad_queries.reshape(seq_len, heads_here, head_size), grad_keys, grad_values)


def on_device(
    tokens,
    pass_ids,
    prefix,
    cotangent,
    qkv_weight,
    out_weight,
    fc1_weight,
    fc2_weight,
    ln1_gain,
    ln1_bias,
    qv_bias,
    out_bias,
    ln2_gain,
    ln2_bias,
    fc1_bias,
    fc2_bias,
    pass_table,
):
    tp_count = lax.axis_size("tp")
    tp_rank = lax.axis_index("tp")
    local_rows = tokens.shape[0]
    seq_len = local_rows * tp_count
    cols_here = qkv_weight.shape[2]
    heads_here = cols_here // HD
    scale = HD ** (-0.5)
    prefix_len = prefix[0]
    gelu_tanh = partial(jax.nn.gelu, approximate=True)
    fsdp_count = lax.axis_size("fsdp")
    qkv_cols = lax.all_gather(qkv_weight, "fsdp", axis=1, tiled=True)
    qkv_full = qkv_cols
    hidden_here = fc1_weight.shape[1]
    qv_here = lax.dynamic_slice_in_dim(qv_bias, tp_rank * cols_here, cols_here, 1)
    one_hot = (pass_ids[:, None] == jnp.arange(NPASS, dtype=jnp.int32)[None, :]).astype(jnp.float32)
    block_in = tokens.astype(jnp.float32) + jnp.dot(
        one_hot, pass_table, precision=HIGH, preferred_element_type=jnp.float32
    )
    normed, unit_one, inv_one = norm_forward(block_in, ln1_gain, ln1_bias)
    normed_all = lax.all_gather(normed.astype(jnp.bfloat16), "tp", axis=0, tiled=True)
    out_pieces = lax.all_gather(out_weight, ("fsdp", "tp"), axis=0, tiled=False)
    out_pieces = out_pieces.reshape((fsdp_count, tp_count) + out_weight.shape)
    out_all = jnp.transpose(out_pieces, (1, 2, 0, 3)).reshape(
        tp_count * out_weight.shape[0], fsdp_count * out_weight.shape[1]
    )
    out_full = lax.dynamic_slice_in_dim(
        out_all, tp_rank * out_weight.shape[0], out_weight.shape[0], 0
    )
    shards = (fc1_weight, fc2_weight)
    packed = jnp.concatenate([piece.reshape(-1) for piece in shards])
    packed, qkv_cols, normed_all = lax.optimization_barrier((packed, qkv_cols, normed_all))
    qkv_full = qkv_cols
    gathered = lax.all_gather(packed, "fsdp", axis=0, tiled=False)
    qkv_all = lax.all_gather(qkv_cols, "tp", axis=2, tiled=True)
    grad_rows = lax.all_gather(cotangent, "tp", axis=0, tiled=True)
    projected = jnp.einsum("rd,kdc->krc", normed_all, qkv_full, preferred_element_type=jnp.float32)
    queries = (projected[0] + qv_here[0]).astype(jnp.bfloat16).reshape(seq_len, heads_here, HD)
    keys_all = projected[1].astype(jnp.bfloat16).reshape(seq_len, heads_here, HD)
    values_all = (projected[2] + qv_here[1]).astype(jnp.bfloat16).reshape(seq_len, heads_here, HD)
    mixed, log_mass = attend_forward(queries, keys_all, values_all, prefix_len, scale)
    mixed, grad_rows, gathered = lax.optimization_barrier((mixed, grad_rows, gathered))
    pieces = []
    offset = 0
    for piece in shards:
        size = piece.size
        pieces.append(gathered[:, offset : offset + size].reshape((fsdp_count,) + piece.shape))
        offset += size
    fc1_part = pieces[0].reshape(-1, fc1_weight.shape[1])
    fc2_part = jnp.moveaxis(pieces[1], 0, 1).reshape(fc2_weight.shape[0], -1)
    mixed_rows = lax.all_to_all(mixed, "tp", 0, 1, tiled=True)
    middle = block_in + jnp.dot(mixed_rows, out_all, preferred_element_type=jnp.float32) + out_bias
    normed_two, unit_two, inv_two = norm_forward(middle, ln2_gain, ln2_bias)
    normed_two = normed_two.astype(jnp.bfloat16)
    grad_top = cotangent.astype(jnp.float32)
    fc1_bias_here = lax.dynamic_slice_in_dim(fc1_bias, tp_rank * hidden_here, hidden_here, 0)
    normed_rows = lax.all_gather(normed_two, "tp", axis=0, tiled=True)
    before = jnp.dot(normed_rows, fc1_part, preferred_element_type=jnp.float32) + fc1_bias_here
    hidden = gelu_tanh(before).astype(jnp.bfloat16)
    fc2_partial = jnp.dot(hidden, fc2_part, preferred_element_type=jnp.float32).astype(jnp.bfloat16)
    grad_hidden = matmul_nt(grad_rows, fc2_part)
    grad_before = jax.vjp(gelu_tanh, before)[1](grad_hidden)[0].astype(jnp.bfloat16)
    grad_fc1_bias = lax.dynamic_update_slice_in_dim(
        jnp.zeros(fc1_bias.shape, jnp.float32),
        jnp.sum(grad_before.astype(jnp.float32), axis=0),
        tp_rank * hidden_here,
        0,
    )
    grad_fc1 = matmul_tn(normed_rows, grad_before)
    grad_fc2 = matmul_tn(hidden, grad_rows)
    grad_normed_two = lax.psum_scatter(
        matmul_nt(grad_before, fc1_part), "tp", scatter_dimension=0, tiled=True
    )
    grad_normed_two, fc2_partial, grad_fc1, grad_fc2 = lax.optimization_barrier(
        (grad_normed_two, fc2_partial, grad_fc1, grad_fc2)
    )
    grad_fc2_bias = jnp.sum(grad_top, axis=0)
    grad_from_norm, grad_ln2_gain, grad_ln2_bias = norm_backward(
        grad_normed_two, unit_two, inv_two, ln2_gain
    )
    grad_middle = grad_top + grad_from_norm
    grad_out_bias = jnp.sum(grad_middle, axis=0)
    grad_attn_rows = lax.all_gather(grad_middle.astype(jnp.bfloat16), "tp", axis=0, tiled=True)
    fc2_partial, grad_attn_rows = lax.optimization_barrier((fc2_partial, grad_attn_rows))
    result = (
        middle
        + lax.psum_scatter(fc2_partial, "tp", scatter_dimension=0, tiled=True).astype(jnp.float32)
        + fc2_bias
    )
    grad_out_w = matmul_tn(mixed, grad_attn_rows)
    fsdp_count = lax.axis_size("fsdp")
    dense_grads = (
        jnp.moveaxis(grad_out_w.reshape(grad_out_w.shape[0], fsdp_count, -1), 1, 0),
        grad_fc1.reshape(fsdp_count, -1, grad_fc1.shape[1]),
        jnp.moveaxis(grad_fc2.reshape(grad_fc2.shape[0], fsdp_count, -1), 1, 0),
    )
    dense_packed = jnp.concatenate([g.reshape(fsdp_count, -1) for g in dense_grads], axis=1)
    dense_summed = lax.psum_scatter(
        dense_packed.reshape(-1, grad_fc1.shape[1]), "fsdp", scatter_dimension=0, tiled=True
    ).reshape(1, -1)
    grad_mixed = (
        matmul_nt(grad_attn_rows, out_full).astype(jnp.bfloat16).reshape(seq_len, heads_here, HD)
    )
    grad_queries, grad_keys, grad_values = attend_backward(
        queries, keys_all, values_all, grad_mixed, log_mass, prefix_len, scale
    )
    grad_q_low = grad_queries.astype(jnp.bfloat16).reshape(seq_len, cols_here)
    grad_k_low = grad_keys.astype(jnp.bfloat16).reshape(seq_len, cols_here)
    grad_v_low = grad_values.astype(jnp.bfloat16).reshape(seq_len, cols_here)
    grad_proj = jnp.stack([grad_q_low, grad_k_low, grad_v_low], axis=1)
    grad_proj, result, dense_summed = lax.optimization_barrier((grad_proj, result, dense_summed))
    dense_shards = []
    offset = 0
    for g in dense_grads:
        size = g[0].size
        dense_shards.append(dense_summed[0, offset : offset + size].reshape(g.shape[1:]))
        offset += size
    out_shard, fc1_shard, fc2_shard = dense_shards
    grad_qv_here = jnp.stack(
        [
            jnp.sum(grad_q_low.astype(jnp.float32), axis=0),
            jnp.sum(grad_v_low.astype(jnp.float32), axis=0),
        ],
        axis=0,
    )
    grad_qv_bias = lax.dynamic_update_slice_in_dim(
        jnp.zeros(qv_bias.shape, jnp.float32), grad_qv_here, tp_rank * cols_here, 1
    )
    grad_qkv_w = jnp.einsum(
        "rd,rkc->kdc", normed_all, grad_proj, preferred_element_type=jnp.float32
    )
    grad_proj_rows = lax.all_to_all(grad_proj, "tp", 0, 2, tiled=True)
    grad_proj_rows, qkv_all = lax.optimization_barrier((grad_proj_rows, qkv_all))
    grad_normed = jnp.einsum(
        "rkc,kdc->rd", grad_proj_rows, qkv_all, preferred_element_type=jnp.float32
    )
    grad_in_norm, grad_ln1_gain, grad_ln1_bias = norm_backward(
        grad_normed, unit_one, inv_one, ln1_gain
    )
    grad_input = grad_middle + grad_in_norm
    grad_table = lax.dot_general(
        one_hot,
        grad_input,
        (((0,), (0,)), ((), ())),
        precision=HIGH,
        preferred_element_type=jnp.float32,
    )
    qkv_shard = lax.psum_scatter(grad_qkv_w, "fsdp", scatter_dimension=1, tiled=True)
    summed = lax.psum(
        (
            grad_ln1_gain,
            grad_ln1_bias,
            grad_qv_bias,
            grad_out_bias,
            grad_ln2_gain,
            grad_ln2_bias,
            grad_fc1_bias,
            grad_fc2_bias,
            grad_table,
        ),
        ("fsdp", "tp"),
    )
    return (
        result.astype(jnp.bfloat16),
        grad_input,
        qkv_shard,
        out_shard,
        fc1_shard,
        fc2_shard,
        summed[0],
        summed[1],
        summed[2],
        summed[3],
        summed[4],
        summed[5],
        summed[6],
        summed[7],
        summed[8],
    )


def solution(mesh):
    placed = (
        P(("fsdp", "tp"), None),
        P(("fsdp", "tp")),
        P("fsdp"),
        P(("fsdp", "tp"), None),
        P(None, "fsdp", "tp"),
        P("tp", "fsdp"),
        P("fsdp", "tp"),
        P("tp", "fsdp"),
        P(),
        P(),
        P(),
        P(),
        P(),
        P(),
        P(),
        P(),
        P(),
    )
    return jax.shard_map(
        on_device,
        mesh=mesh,
        in_specs=placed,
        out_specs=(
            P(("fsdp", "tp"), None),
            P(("fsdp", "tp"), None),
            P(None, "fsdp", "tp"),
            P("tp", "fsdp"),
            P("fsdp", "tp"),
            P("tp", "fsdp"),
            P(),
            P(),
            P(),
            P(),
            P(),
            P(),
            P(),
            P(),
            P(),
        ),
        check_vma=False,
    )
```

profile of v0, /device:TPU:0, one launch (start us, length us, event | category | flops | bytes accessed | tf_op | source)
XLA Modules:
  0.0 645.1 jit_solution(12459462399136723489)
XLA Ops:
  13.2 38.9 %all_gather.30 = bf16[3,768,192]{2,0,1:T(4,128)(2,1)S(1)} all-gather(bf16[3,96,192]{2,0,1:T(4,128)(2,1)S(1)} %copy.92), channel_id=1, replica_groups=mesh['fsdp'=8,'tp'=4] {'fsdp'}, dimensions={1}, use_global_device_ids=true | all-gather | bytes 995328 | tf_op jit(solution)/shard_map/all_gather | solution.py:145
  56.2 4.2 convolution_bitcast_fusion
  66.7 89.5 %while.27 = (s32[]{:T(128)}, bf16[4,512,3,64]{1,3,2,0:T(8,128)(2,1)S(1)}, f32[4,3,512]{2,1,0:T(4,128)S(1)}, s32[4]{0:T(128)S(1)}, s32[]{:T(128)}, /*index=5*/bf1...) while((s32[]{:T(128)}, ...), condition=%wide.region_5.6_spmd, body=%wide.region_2.5_spmd.sunk | while | flops 845251584 | bytes 43976836 | solution.py:71
  69.3 6.1 fusion.129
  75.4 6.9 %fusion.130 = f32[3,512]{1,0:T(4,128)S(1)} fusion(f32[3,512,2048]{2,1,0:T(8,128)} %get-tuple-element.513, f32[3,512]{1,0:T(4,128)S(1)} %get-tuple-element.514, pred[512,2048]{1,0:T(8,128)(4,1)S(1)} %fusion.128), kind=kLoop, calls=%fused_computation.4.clone.1 | loop fusion | flops 12581376 | bytes 13643776 | tf_op jit(solution)/shard_map/while/body/eval_jaxpr/reduce_sum | solution.py:64
  82.3 6.8 %fusion.131 = bf16[4,512,3,64]{1,3,2,0:T(8,128)(2,1)S(1)} fusion(bf16[4,512,3,64]{1,3,2,0:T(8,128)(2,1)S(1)} %get-tuple-element.538, s32[]{:T(128)S(6)} %copy.135, bf16[2048,3,64]{0,2,1:T(8,128)(2,1)S(1)} %get-tuple-element.553, f32[3,512,2048]{2,1,0:T(8,128)} %get-tuple-element.513, f32[3,512]{1,0:T(4,128)S(1)} %fusion.130, ...), kind=kOutput, calls=%fused_computation.10.clone.1 | convolution fusion | flops 418480128 | bytes 14630916 | tf_op jit(solution)/shard_map/while/body/eval_jaxpr/hqk,khe->qhe/dot_general | solution.py:66
  91.8 6.1 fusion.129
  97.9 6.8 %fusion.130 = f32[3,512]{1,0:T(4,128)S(1)} fusion(f32[3,512,2048]{2,1,0:T(8,128)} %get-tuple-element.513, f32[3,512]{1,0:T(4,128)S(1)} %get-tuple-element.514, pred[512,2048]{1,0:T(8,128)(4,1)S(1)} %fusion.128), kind=kLoop, calls=%fused_computation.4.clone.1 | loop fusion | flops 12581376 | bytes 13643776 | tf_op jit(solution)/shard_map/while/body/eval_jaxpr/reduce_sum | solution.py:64
  104.6 6.8 %fusion.131 = bf16[4,512,3,64]{1,3,2,0:T(8,128)(2,1)S(1)} fusion(bf16[4,512,3,64]{1,3,2,0:T(8,128)(2,1)S(1)} %get-tuple-element.538, s32[]{:T(128)S(6)} %copy.135, bf16[2048,3,64]{0,2,1:T(8,128)(2,1)S(1)} %get-tuple-element.553, f32[3,512,2048]{2,1,0:T(8,128)} %get-tuple-element.513, f32[3,512]{1,0:T(4,128)S(1)} %fusion.130, ...), kind=kOutput, calls=%fused_computation.10.clone.1 | convolution fusion | flops 418480128 | bytes 14630916 | tf_op jit(solution)/shard_map/while/body/eval_jaxpr/hqk,khe->qhe/dot_general | solution.py:66
  114.1 6.1 fusion.129
  120.2 6.8 %fusion.130 = f32[3,512]{1,0:T(4,128)S(1)} fusion(f32[3,512,2048]{2,1,0:T(8,128)} %get-tuple-element.513, f32[3,512]{1,0:T(4,128)S(1)} %get-tuple-element.514, pred[512,2048]{1,0:T(8,128)(4,1)S(1)} %fusion.128), kind=kLoop, calls=%fused_computation.4.clone.1 | loop fusion | flops 12581376 | bytes 13643776 | tf_op jit(solution)/shard_map/while/body/eval_jaxpr/reduce_sum | solution.py:64
  127.0 6.8 %fusion.131 = bf16[4,512,3,64]{1,3,2,0:T(8,128)(2,1)S(1)} fusion(bf16[4,512,3,64]{1,3,2,0:T(8,128)(2,1)S(1)} %get-tuple-element.538, s32[]{:T(128)S(6)} %copy.135, bf16[2048,3,64]{0,2,1:T(8,128)(2,1)S(1)} %get-tuple-element.553, f32[3,512,2048]{2,1,0:T(8,128)} %get-tuple-element.513, f32[3,512]{1,0:T(4,128)S(1)} %fusion.130, ...), kind=kOutput, calls=%fused_computation.10.clone.1 | convolution fusion | flops 418480128 | bytes 14630916 | tf_op jit(solution)/shard_map/while/body/eval_jaxpr/hqk,khe->qhe/dot_general | solution.py:66
  136.5 6.1 fusion.129
  142.6 6.8 %fusion.130 = f32[3,512]{1,0:T(4,128)S(1)} fusion(f32[3,512,2048]{2,1,0:T(8,128)} %get-tuple-element.513, f32[3,512]{1,0:T(4,128)S(1)} %get-tuple-element.514, pred[512,2048]{1,0:T(8,128)(4,1)S(1)} %fusion.128), kind=kLoop, calls=%fused_computation.4.clone.1 | loop fusion | flops 12581376 | bytes 13643776 | tf_op jit(solution)/shard_map/while/body/eval_jaxpr/reduce_sum | solution.py:64
  149.4 6.8 %fusion.131 = bf16[4,512,3,64]{1,3,2,0:T(8,128)(2,1)S(1)} fusion(bf16[4,512,3,64]{1,3,2,0:T(8,128)(2,1)S(1)} %get-tuple-element.538, s32[]{:T(128)S(6)} %copy.135, bf16[2048,3,64]{0,2,1:T(8,128)(2,1)S(1)} %get-tuple-element.553, f32[3,512,2048]{2,1,0:T(8,128)} %get-tuple-element.513, f32[3,512]{1,0:T(4,128)S(1)} %fusion.130, ...), kind=kOutput, calls=%fused_computation.10.clone.1 | convolution fusion | flops 418480128 | bytes 14630916 | tf_op jit(solution)/shard_map/while/body/eval_jaxpr/hqk,khe->qhe/dot_general | solution.py:66
  157.0 4.4 reshape.280
  162.4 4.2 all-to-all-start
  167.6 22.4 %all-gather.22.cloned.1.call-done = bf16[6144,96]{1,0:T(8,128)(2,1)} async-done(((bf16[192,96]{1,0:T(8,128)(2,1)}), bf16[6144,96]{1,0:T(8,128)(2,1)}) %all-gather.22.cloned.1.call-update) | async-done | bytes 1179664 | tf_op jit(solution)/shard_map/all_gather | solution.py:155
  199.1 3.3 fusion.68
  208.1 3.7 reshape.270
  214.3 12.4 %all-gather.14.cloned.1.call-done = bf16[2048,768]{1,0:T(8,128)(2,1)} async-done(((bf16[512,768]{1,0:T(8,128)(2,1)}), bf16[2048,768]{1,0:T(8,128)(2,1)}) %all-gather.14.cloned.1.call-update) | async-done | bytes 3145744 | tf_op jit(solution)/shard_map/all_gather | solution.py:190
  226.7 5.1 fusion.71
  231.8 8.3 %convert_reduce_fusion = (f32[768]{0:T(1024)}, bf16[2048,768]{1,0:T(8,128)(2,1)S(1)}, bf16[2048,768]{1,0:T(8,128)(2,1)}) fusion(f32[2048,768]{1,0:T(8,128)S(1)} %fusion.71, f32[768]{0:T(1024)S(1)} %dynamic_slice.31, bf16[2048,768]{1,0:T(8,128)(2,1)S(1)} %copy-done.48, bf16[768,768]{0,1:T(8,128)(2,1)S(1)} %bitcast.200), kind=kOutput, calls=%fused_computation.64 | convolution fusion | flops 2455239936 | bytes 16914432 | tf_op jit(solution)/shard_map/dot_general | solution.py:31
  241.9 4.6 fusion.72
  246.9 6.6 %convolution_convert_fusion = bf16[2048,768]{1,0:T(8,128)(2,1)} fusion(bf16[2048,768]{1,0:T(8,128)(2,1)} %get-tuple-element.391, bf16[768,768]{0,1:T(8,128)(2,1)} %bitcast.199), kind=kOutput, calls=%fused_computation.67 | convolution fusion | flops 2417491968 | bytes 7471104 | tf_op jit(solution)/shard_map/dot_general | solution.py:193
  253.6 8.6 %fusion.74 = f32[768,768]{1,0:T(8,128)} fusion(bf16[2048,768]{1,0:T(8,128)(2,1)} %get-tuple-element.391, bf16[2048,768]{1,0:T(8,128)(2,1)} %all-gather.12.cloned.1.call-done), kind=kOutput, calls=%fused_computation.134 | convolution fusion | flops 2415919104 | bytes 8650752 | tf_op jit(solution)/shard_map/dot_general | solution.py:37
  262.2 4.1 fusion.73
  266.3 39.1 %reduce-scatter.7.cloned.1.call-done = f32[512,768]{1,0:T(8,128)} async-done(((f32[2048,768]{1,0:T(8,128)}), f32[512,768]{1,0:T(8,128)}) %reduce-scatter.7.cloned.1.call-update) | async-done | bytes 1572880 | tf_op jit(solution)/shard_map/reduce_scatter | solution.py:204
  311.9 3.5 reshape_reshape.13
  315.4 3.1 copy.102
  318.5 3.6 copy.103
  322.0 5.2 reshape.277
  327.2 13.3 %all-gather.16.cloned.1.call-done = bf16[2048,768]{1,0:T(8,128)(2,1)} async-done(((bf16[512,768]{1,0:T(8,128)(2,1)}), bf16[2048,768]{1,0:T(8,128)(2,1)}) %all-gather.16.cloned.1.call-update) | async-done | bytes 3145744 | tf_op jit(solution)/shard_map/all_gather | solution.py:216
  344.2 5.1 pad_maximum_fusion
  349.3 6.4 reshape.278
  356.4 3.1 convolution_convert_fusion.1
  360.2 137.4 %while.28 = (s32[]{:T(128)}, f32[2048,3,64]{0,2,1:T(8,128)}, f32[2048,3,64]{0,2,1:T(8,128)}, bf16[4,512,3,64]{1,3,2,0:T(8,128)(2,1)}, bf16[4,512,3,64]{1,3,2,0:T...) while((s32[]{:T(128)}, f32[2048,3,64]{0,2,1:T(8,128)}, ...), condition=%wide.region_13.14_spmd.clone, body=%wide.region_11.13_spmd.clone.sunk | while | flops 2064614400 | bytes 156684720 | solution.py:110
  366.3 4.9 fusion.144
  371.2 6.2 multiply_reduce_fusion.8
  377.4 6.3 multiply_convert_fusion.3
  383.7 5.8 fusion.145
  389.5 3.6 fusion.143
  399.0 6.3 fusion.144
  405.3 6.2 multiply_reduce_fusion.8
  411.5 6.3 multiply_convert_fusion.3
  417.8 5.9 fusion.145
  423.7 4.2 fusion.143
  433.8 6.4 fusion.144
  440.2 6.2 multiply_reduce_fusion.8
  446.3 6.3 multiply_convert_fusion.3
  452.6 5.8 fusion.145
  458.5 4.2 fusion.143
  468.5 6.3 fusion.144
  474.9 6.2 multiply_reduce_fusion.8
  481.0 6.3 multiply_convert_fusion.3
  487.3 5.9 fusion.145
  493.2 4.2 fusion.143
  509.0 5.9 fusion.56
  520.7 7.0 %copy.104 = bf16[2048,3,192]{2,1,0:T(4,128)(2,1)} copy(bf16[2048,3,192]{0,2,1:T(8,128)(2,1)} %pad_maximum_fusion.1) | data formatting | bytes 4718592 | tf_op jit(solution)/shard_map/optimization_barrier | solution.py:244
  527.7 5.0 all-to-all-start.1
  537.8 43.1 %all-to-all-done.1 = bf16[2048,3,192]{2,1,0:T(4,128)(2,1)} async-done(((bf16[2048,3,192]{2,1,0:T(4,128)(2,1)}), bf16[2048,3,192]{2,1,0:T(4,128)(2,1)}, u32[]{:S(2)}, u32[]{:S(2)}) %all-to-all-start.1) | async-done | bytes 2359328 | tf_op jit(solution)/shard_map/all_to_all | solution.py:265
  581.0 7.2 %copy.106 = bf16[512,3,4,192]{0,3,2,1:T(8,128)(2,1)} copy(bf16[512,3,4,192]{3,1,0,2:T(4,128)(2,1)} %bitcast.23) | data formatting | bytes 4718592 | tf_op jit(solution)/shard_map/all_to_all | solution.py:265
  588.1 5.4 fusion.54
  595.0 41.4 %all-reduce = (f32[768]{0:T(1024)}, f32[768]{0:T(1024)}, f32[2,768]{1,0:T(2,128)}, f32[768]{0:T(1024)}, f32[768]{0:T(1024)}, /*index=5*/f32[768]{0:T(1024)}, f32[3072]{0:T(1024)}, f32[768]{0:T(1024)}, f32[5,768]{1,0:T(8,128)}) all-reduce(f32[768]{0:T(1024)S(1)} %get-tuple-element.324, ...), channel_id=1, replica_groups=mesh['fsdp'=8,'tp'=4] {'fsdp','tp'}, use_global_device_ids=true, to_apply=%region_20.21 | all-reduce | flops 13056 | bytes 104448 | tf_op jit(solution)/shard_map/psum | solution.py:282
  (306 shorter events, 109.1 us)
Async XLA Ops:
  7.2 4.0 copy-start.41
  7.2 4.0 copy-start.44
  7.2 45.7 %all-gather.10.cloned.1.call-start = ((), (), s32[]{:S(2)}) async-start(), calls=%async_computation.6 | async-start | bytes 3932160 | tf_op jit(solution)/shard_map/all_gather | solution.py:154
  11.2 41.0 %copy-start.35 = (f32[512]{0:T(512)}, f32[512]{0:T(512)S(1)}, u32[]{:S(2)}) copy-start(f32[512]{0:T(512)S(1)} %add_rsqrt_fusion.1) | copy-start | bytes 6148
  12.4 144.6 %all-gather.20.cloned.1.call-start = ((), (), s32[]{:S(2)}) async-start(), calls=%async_computation.14 | async-start | bytes 2654208 | tf_op jit(solution)/shard_map/all_gather | solution.py:167
  52.9 108.5 %all-gather.12.cloned.1.call-start = ((), (), s32[]{:S(2)}) async-start(), calls=%async_computation.7 | async-start | bytes 3932160 | tf_op jit(solution)/shard_map/all_gather | solution.py:169
  53.7 136.3 %all-gather.22.cloned.1.call-start = ((), (), s32[]{:S(2)}) async-start(), calls=%async_computation.15 | async-start | bytes 1622016 | tf_op jit(solution)/shard_map/all_gather | solution.py:155
  56.2 4.2 copy-start.22
  156.2 5.2 copy-start.14
  157.0 4.4 copy-start.15
  162.4 32.2 %all-to-all-start = ((bf16[4,512,192]{1,2,0:T(8,128)(2,1)}), bf16[4,512,192]{1,2,0:T(8,128)(2,1)}, u32[]{:S(2)}, u32[]{:S(2)}) async-start(bf16[4,512,192]{1,2,0:T(8,128)(2,1)} %bitcast.141), calls=%async_computation | async-start | bytes 1572864 | tf_op jit(solution)/shard_map/all_to_all | solution.py:184
  166.6 60.2 %all-gather.14.cloned.1.call-start = ((), (), s32[]{:S(2)}) async-start(), calls=%async_computation.8 | async-start | bytes 3932160 | tf_op jit(solution)/shard_map/all_gather | solution.py:190
  190.0 4.6 copy-start.50
  197.5 110.9 %copy-start.8 = (f32[512,768]{1,0:T(8,128)}, f32[512,768]{1,0:T(8,128)S(1)}, u32[]{:S(2)}) copy-start(f32[512,768]{1,0:T(8,128)S(1)} %get-tuple-element.400) | copy-start | bytes 4718596
  199.1 106.4 %reduce-scatter.7.cloned.1.call-start = ((), (), s32[]{:S(2)}) async-start(), calls=%async_computation.9 | async-start | bytes 7864320 | tf_op jit(solution)/shard_map/reduce_scatter | solution.py:204
  226.7 5.1 copy-start.28
  226.7 5.1 copy-start.48
  231.8 10.1 %copy-start.27 = (bf16[768,768]{1,0:T(8,128)(2,1)S(1)}, bf16[768,768]{1,0:T(8,128)(2,1)}, u32[]{:S(2)}) copy-start(bf16[768,768]{1,0:T(8,128)(2,1)} %reshape_reshape.11) | copy-start | bytes 3538948
  246.5 94.0 %all-gather.16.cloned.1.call-start = ((), (), s32[]{:S(2)}) async-start(), calls=%async_computation.10 | async-start | bytes 3932160 | tf_op jit(solution)/shard_map/all_gather | solution.py:216
  253.6 8.7 %copy-start.49 = (bf16[2048,768]{1,0:T(8,128)(2,1)S(1)}, bf16[2048,768]{1,0:T(8,128)(2,1)}, u32[]{:S(2)}) copy-start(bf16[2048,768]{1,0:T(8,128)(2,1)} %all-gather.14.cloned.1.call-done) | copy-start | bytes 9437188
  253.6 8.7 %copy-start.52 = (bf16[2048,768]{1,0:T(8,128)(2,1)S(1)}, bf16[2048,768]{1,0:T(8,128)(2,1)}, u32[]{:S(2)}) copy-start(bf16[2048,768]{1,0:T(8,128)(2,1)} %copy-done.51) | copy-start | bytes 9437188
  311.8 192.1 %reduce-scatter.9.cloned.1.call-start = ((), (), s32[]{:S(2)}) async-start(), calls=%async_computation.11 | async-start | bytes 3932160 | tf_op jit(solution)/shard_map/reduce_scatter | solution.py:220
  322.0 18.5 %copy-start.16 = (bf16[24,8,4,512]{3,1,2,0:T(8,128)(2,1)S(1)}, bf16[24,8,4,512]{3,1,2,0:T(8,128)(2,1)}, u32[]{:S(2)}) copy-start(bf16[24,8,4,512]{3,1,2,0:T(8,128)(2,1)} %copy-done.15) | copy-start | bytes 2359300
  343.2 163.1 %reduce-scatter.11.cloned.1.call-start = ((), (), s32[]{:S(2)}) async-start(), calls=%async_computation.12 | async-start | bytes 5971968 | tf_op jit(solution)/shard_map/reduce_scatter | solution.py:231
  355.7 232.4 %all-gather.18.cloned.1.call-start = ((), (), s32[]{:S(2)}) async-start(), calls=%async_computation.13 | async-start | bytes 4423680 | tf_op jit(solution)/shard_map/all_gather | solution.py:168
  356.3 280.1 %reduce-scatter.13.cloned.1.call-start = ((), (), s32[]{:S(2)}) async-start(), calls=%async_computation.16 | async-start | bytes 2211840
  360.4 5.9 copy-start.4
  360.4 5.9 copy-start.6
  360.4 5.9 copy-start.20
  383.7 5.8 copy-start.2
  389.5 3.6 copy-start.7
  389.5 3.6 copy-start.21
  393.1 5.9 copy-start.4
  393.1 5.9 copy-start.6
  393.1 5.9 copy-start.20
  417.8 5.9 copy-start.2
  423.7 4.2 copy-start.5
  423.7 4.2 copy-start.7
  423.7 4.2 copy-start.21
  427.9 5.9 copy-start.4
  427.9 5.9 copy-start.6
  427.9 5.9 copy-start.20
  452.6 5.8 copy-start.2
  458.4 4.2 copy-start.5
  458.4 4.2 copy-start.7
  458.4 4.2 copy-start.21
  462.6 5.9 copy-start.4
  462.7 5.9 copy-start.6
  462.7 5.9 copy-start.20
  487.3 5.9 copy-start.2
  493.2 4.2 copy-start.5
  493.2 4.2 copy-start.7
  493.2 4.2 copy-start.21
  527.7 5.1 copy-start.47
  527.7 5.4 copy-start.25
  527.7 5.9 copy-start.26
  527.7 53.2 %all-to-all-start.1 = ((bf16[2048,3,192]{2,1,0:T(4,128)(2,1)}), bf16[2048,3,192]{2,1,0:T(4,128)(2,1)}, u32[]{:S(2)}, u32[]{:S(2)}) async-start(bf16[2048,3,192]{2,1,0:T(4,128)(2,1)} %copy.104), calls=%async_computation.4 | async-start | bytes 8388608 | tf_op jit(solution)/shard_map/all_to_all | solution.py:265
  580.9 7.2 %copy-start.11 = (f32[512,768]{1,0:T(8,128)S(1)}, f32[512,768]{1,0:T(8,128)}, u32[]{:S(2)}) copy-start(f32[512,768]{1,0:T(8,128)} %copy-done.10) | copy-start | bytes 4718596
  580.9 7.2 %copy-start.34 = (f32[512]{0:T(512)S(1)}, f32[512]{0:T(512)}, u32[]{:S(2)}) copy-start(f32[512]{0:T(512)} %copy-done.33) | copy-start | bytes 6148
  580.9 7.2 %copy-start.36 = (f32[512]{0:T(512)S(1)}, f32[512]{0:T(512)}, u32[]{:S(2)}) copy-start(f32[512]{0:T(512)} %copy-done.35) | copy-start | bytes 6148
  581.0 7.2 %copy-start.42 = (f32[768]{0:T(1024)S(1)}, f32[768]{0:T(1024)}, u32[]{:S(2)}) copy-start(f32[768]{0:T(1024)} %param.29) | copy-start | bytes 9220
  588.1 5.4 copy-start.13
  593.7 44.7 %copy-start.1 = (f32[5,768]{1,0:T(8,128)S(1)}, f32[5,768]{1,0:T(8,128)}, u32[]{:S(2)}) copy-start(f32[5,768]{1,0:T(8,128)} %param.37) | copy-start | bytes 46084
  594.3 44.1 %copy-start.17 = (f32[512,768]{1,0:T(8,128)}, f32[512,768]{1,0:T(8,128)S(1)}, u32[]{:S(2)}) copy-start(f32[512,768]{1,0:T(8,128)S(1)} %multiply_add_fusion) | copy-start | bytes 4718596
  (26 other events, 56.6 us)
Sparse Core Ops, SparseCore 0:
  12.5 31.2 all-gather.9
  53.0 50.5 all-gather.19
  105.2 27.0 all-gather.11
  135.0 54.9 all-gather.21
  199.2 27.4 all-gather.13
  246.6 58.8 reduce-scatter.6
  312.0 28.4 all-gather.15
  343.4 37.8 reduce-scatter.8
  384.9 104.4 reduce-scatter.10
  490.8 30.3 all-gather.17
  524.7 67.3 reduce-scatter.12
where the time goes:
time: 650 us; the launch traced here: 645 us
  matrix products  216 us (33%)
  waiting for transfers between devices  132 us (20%)
  local copies, waits for them, and re-layouts  97.2 us (15%)
  other arithmetic  93.3 us (14%)
  blocking collectives  80.3 us (12%)
  between operations  14.8 us (2%)
  starting transfers between devices  10.7 us (2%)
    all_to_all x1, waiting for transfers between devices, on_device(): grad_proj_rows = lax.all_to_all(grad_proj, 'tp', 0, 2, tiled=True)  43.1 us
    psum x1, blocking collectives, on_device(): lax.psum((grad_ln1_gain, grad_ln1_bias, grad_qv_bias, grad_out_bias, grad...  41.4 us
    reduce_scatter x1, waiting for transfers between devices, on_device(): lax.psum_scatter(matmul_nt(grad_before, fc1_part), 'tp', scatter_dimensio...  39.1 us
    all_gather x1, blocking collectives, on_device(): qkv_cols = lax.all_gather(qkv_weight, 'fsdp', axis=1, tiled=True)  38.9 us
    dot_general x8, matrix products, block_scores(): jnp.einsum('qhe,khe->hqk', query_block, keys_all, preferred_element_type=...  36.4 us
    reduce_sum x4, other arithmetic, one_block(): total_mass = jnp.sum(expo, axis=-1, keepdims=True)  27.2 us
    dot_general x4, matrix products, one_block(): jnp.einsum('hqk,khe->qhe', probs_low, values_all, preferred_element_type=...  27.1 us
    convert_element_type x4, other arithmetic, one_block(): grad_scores = (probs * (grad_probs - inner_sum)).astype(jnp.bfloat16)  25.2 us
  transfers between devices with their start and end apart: 13, of which 5 were waited for; matrix products, arithmetic and copies ran while one was open for 57% of the time, Pallas kernels for 0%

commit v1 on v0

--- a/solution.py
+++ b/solution.py
@@ -1,3 +1,4 @@
+import functools
 from functools import partial
 import jax
 import jax.numpy as jnp
@@ -10,6 +11,21 @@
 HIGH = lax.Precision.HIGHEST
 EPS = 1e-05
 NEG_FILL = -1e30
+
+
+def shards_review(unit, axis_name, join_dim, where_dim):
+    return jnp.concatenate(
+        jax.lax.all_to_all(
+            jnp.stack(jnp.split(unit, jax.lax.psum(1, axis_name=axis_name), axis=join_dim)),
+            concat_axis=0,
+            split_axis=0,
+            axis_name=axis_name,
+        ),
+        axis=where_dim,
+    )
+
+
+unite_local_data = functools.partial(shards_review, axis_name="tp", join_dim=0, where_dim=2)
 
 
 def norm_forward(rows_in, gain, shift):
@@ -262,7 +278,7 @@
     grad_qkv_w = jnp.einsum(
         "rd,rkc->kdc", normed_all, grad_proj, preferred_element_type=jnp.float32
     )
-    grad_proj_rows = lax.all_to_all(grad_proj, "tp", 0, 2, tiled=True)
+    grad_proj_rows = unite_local_data(grad_proj)
     grad_proj_rows, qkv_all = lax.optimization_barrier((grad_proj_rows, qkv_all))
     grad_normed = jnp.einsum(
         "rkc,kdc->rd", grad_proj_rows, qkv_all, preferred_element_type=jnp.float32

time: 650 us -> 624 us (0.960)
  waiting for transfers between devices: 132 us -> 110 us
    all_to_all x1, waiting for transfers between devices: 43.1 us -> 21.2 us  [shards_review(): jax.lax.all_to_all(jnp.stack(jnp.split(unit, jax.lax.psum(1, axis_name=ax...]
    all_to_all x1 -> x0, local copies, waits for them, and re-layouts: 7.15 us -> none  [on_device(): grad_proj_rows = lax.all_to_all(grad_proj, 'tp', 0, 2, tiled=True)]
    optimization_barrier x1 -> x0, local copies, waits for them, and re-layouts: 6.96 us -> none  [on_device(): lax.optimization_barrier((grad_proj, result, dense_summed))]
  transfers between devices with their start and end apart: 13 -> 13, of which waited for: 5 -> 5; matrix products, arithmetic and copies ran while one was open for 57% -> 58% of each run, Pallas kernels for 0% -> 0%
where the time goes in v1:
time: 624 us; the launch traced here: 619 us
  matrix products  216 us (35%)
  waiting for transfers between devices  110 us (18%)
  other arithmetic  95.2 us (15%)
  local copies, waits for them, and re-layouts  91.9 us (15%)
  blocking collectives  80.6 us (13%)
  between operations  14.8 us (2%)
  starting transfers between devices  9.46 us (2%)
    psum x1, blocking collectives, on_device(): lax.psum((grad_ln1_gain, grad_ln1_bias, grad_qv_bias, grad_out_bias, grad...  41.7 us
    reduce_scatter x1, waiting for transfers between devices, on_device(): lax.psum_scatter(matmul_nt(grad_before, fc1_part), 'tp', scatter_dimensio...  39.1 us
    all_gather x1, blocking collectives, on_device(): qkv_cols = lax.all_gather(qkv_weight, 'fsdp', axis=1, tiled=True)  38.9 us
    dot_general x8, matrix products, block_scores(): jnp.einsum('qhe,khe->hqk', query_block, keys_all, preferred_element_type=...  36.4 us
    reduce_sum x4, other arithmetic, one_block(): total_mass = jnp.sum(expo, axis=-1, keepdims=True)  27.3 us
    dot_general x4, matrix products, one_block(): jnp.einsum('hqk,khe->qhe', probs_low, values_all, preferred_element_type=...  27.1 us
    convert_element_type x4, other arithmetic, one_block(): grad_scores = (probs * (grad_probs - inner_sum)).astype(jnp.bfloat16)  25.3 us
    dot_general x4, matrix products, one_block(): jnp.einsum('qhe,khe->hqk', grad_block, values_all, preferred_element_type...  24.6 us
  transfers between devices with their start and end apart: 13, of which 5 were waited for; matrix products, arithmetic and copies ran while one was open for 58% of the time, Pallas kernels for 0%

profile of v1, /device:TPU:0, one launch (start us, length us, event | category | flops | bytes accessed | tf_op | source)
XLA Modules:
  0.0 618.9 jit_solution(5381323511607898488)
XLA Ops:
  13.2 38.9 %all_gather.30 = bf16[3,768,192]{2,0,1:T(4,128)(2,1)S(1)} all-gather(bf16[3,96,192]{2,0,1:T(4,128)(2,1)S(1)} %copy.72), channel_id=1, replica_groups=mesh['fsdp'=8,'tp'=4] {'fsdp'}, dimensions={1}, use_global_device_ids=true | all-gather | bytes 995328 | tf_op jit(solution)/shard_map/all_gather | solution.py:161
  56.2 4.2 convolution_bitcast_fusion
  66.7 89.6 %while.27 = (s32[]{:T(128)}, bf16[4,512,3,64]{1,3,2,0:T(8,128)(2,1)S(1)}, f32[4,3,512]{2,1,0:T(4,128)S(1)}, s32[4]{0:T(128)S(1)}, s32[]{:T(128)}, /*index=5*/bf1...) while((s32[]{:T(128)}, ...), condition=%wide.region_5.6_spmd, body=%wide.region_2.5_spmd.sunk | while | flops 845251584 | bytes 43976836 | solution.py:87
  69.4 6.1 fusion.129
  75.4 7.0 %fusion.130 = f32[3,512]{1,0:T(4,128)S(1)} fusion(f32[3,512,2048]{2,1,0:T(8,128)} %get-tuple-element.491, f32[3,512]{1,0:T(4,128)S(1)} %get-tuple-element.492, pred[512,2048]{1,0:T(8,128)(4,1)S(1)} %fusion.128), kind=kLoop, calls=%fused_computation.4.clone.1 | loop fusion | flops 12581376 | bytes 13643776 | tf_op jit(solution)/shard_map/while/body/eval_jaxpr/reduce_sum | solution.py:80
  82.4 6.8 %fusion.131 = bf16[4,512,3,64]{1,3,2,0:T(8,128)(2,1)S(1)} fusion(bf16[4,512,3,64]{1,3,2,0:T(8,128)(2,1)S(1)} %get-tuple-element.516, s32[]{:T(128)S(6)} %copy.111, bf16[2048,3,64]{0,2,1:T(8,128)(2,1)S(1)} %get-tuple-element.531, f32[3,512,2048]{2,1,0:T(8,128)} %get-tuple-element.491, f32[3,512]{1,0:T(4,128)S(1)} %fusion.130, ...), kind=kOutput, calls=%fused_computation.10.clone.1 | convolution fusion | flops 418480128 | bytes 14630916 | tf_op jit(solution)/shard_map/while/body/eval_jaxpr/hqk,khe->qhe/dot_general | solution.py:82
  91.9 6.1 fusion.129
  98.0 6.8 %fusion.130 = f32[3,512]{1,0:T(4,128)S(1)} fusion(f32[3,512,2048]{2,1,0:T(8,128)} %get-tuple-element.491, f32[3,512]{1,0:T(4,128)S(1)} %get-tuple-element.492, pred[512,2048]{1,0:T(8,128)(4,1)S(1)} %fusion.128), kind=kLoop, calls=%fused_computation.4.clone.1 | loop fusion | flops 12581376 | bytes 13643776 | tf_op jit(solution)/shard_map/while/body/eval_jaxpr/reduce_sum | solution.py:80
  104.7 6.8 %fusion.131 = bf16[4,512,3,64]{1,3,2,0:T(8,128)(2,1)S(1)} fusion(bf16[4,512,3,64]{1,3,2,0:T(8,128)(2,1)S(1)} %get-tuple-element.516, s32[]{:T(128)S(6)} %copy.111, bf16[2048,3,64]{0,2,1:T(8,128)(2,1)S(1)} %get-tuple-element.531, f32[3,512,2048]{2,1,0:T(8,128)} %get-tuple-element.491, f32[3,512]{1,0:T(4,128)S(1)} %fusion.130, ...), kind=kOutput, calls=%fused_computation.10.clone.1 | convolution fusion | flops 418480128 | bytes 14630916 | tf_op jit(solution)/shard_map/while/body/eval_jaxpr/hqk,khe->qhe/dot_general | solution.py:82
  114.2 6.1 fusion.129
  120.3 6.8 %fusion.130 = f32[3,512]{1,0:T(4,128)S(1)} fusion(f32[3,512,2048]{2,1,0:T(8,128)} %get-tuple-element.491, f32[3,512]{1,0:T(4,128)S(1)} %get-tuple-element.492, pred[512,2048]{1,0:T(8,128)(4,1)S(1)} %fusion.128), kind=kLoop, calls=%fused_computation.4.clone.1 | loop fusion | flops 12581376 | bytes 13643776 | tf_op jit(solution)/shard_map/while/body/eval_jaxpr/reduce_sum | solution.py:80
  127.1 6.8 %fusion.131 = bf16[4,512,3,64]{1,3,2,0:T(8,128)(2,1)S(1)} fusion(bf16[4,512,3,64]{1,3,2,0:T(8,128)(2,1)S(1)} %get-tuple-element.516, s32[]{:T(128)S(6)} %copy.111, bf16[2048,3,64]{0,2,1:T(8,128)(2,1)S(1)} %get-tuple-element.531, f32[3,512,2048]{2,1,0:T(8,128)} %get-tuple-element.491, f32[3,512]{1,0:T(4,128)S(1)} %fusion.130, ...), kind=kOutput, calls=%fused_computation.10.clone.1 | convolution fusion | flops 418480128 | bytes 14630916 | tf_op jit(solution)/shard_map/while/body/eval_jaxpr/hqk,khe->qhe/dot_general | solution.py:82
  136.6 6.1 fusion.129
  142.7 6.8 %fusion.130 = f32[3,512]{1,0:T(4,128)S(1)} fusion(f32[3,512,2048]{2,1,0:T(8,128)} %get-tuple-element.491, f32[3,512]{1,0:T(4,128)S(1)} %get-tuple-element.492, pred[512,2048]{1,0:T(8,128)(4,1)S(1)} %fusion.128), kind=kLoop, calls=%fused_computation.4.clone.1 | loop fusion | flops 12581376 | bytes 13643776 | tf_op jit(solution)/shard_map/while/body/eval_jaxpr/reduce_sum | solution.py:80
  149.5 6.8 %fusion.131 = bf16[4,512,3,64]{1,3,2,0:T(8,128)(2,1)S(1)} fusion(bf16[4,512,3,64]{1,3,2,0:T(8,128)(2,1)S(1)} %get-tuple-element.516, s32[]{:T(128)S(6)} %copy.111, bf16[2048,3,64]{0,2,1:T(8,128)(2,1)S(1)} %get-tuple-element.531, f32[3,512,2048]{2,1,0:T(8,128)} %get-tuple-element.491, f32[3,512]{1,0:T(4,128)S(1)} %fusion.130, ...), kind=kOutput, calls=%fused_computation.10.clone.1 | convolution fusion | flops 418480128 | bytes 14630916 | tf_op jit(solution)/shard_map/while/body/eval_jaxpr/hqk,khe->qhe/dot_general | solution.py:82
  157.1 4.4 reshape.288
  162.5 4.2 all-to-all-start
  167.7 22.4 %all-gather.22.cloned.1.call-done = bf16[6144,96]{1,0:T(8,128)(2,1)} async-done(((bf16[192,96]{1,0:T(8,128)(2,1)}), bf16[6144,96]{1,0:T(8,128)(2,1)}) %all-gather.22.cloned.1.call-update) | async-done | bytes 1179664 | tf_op jit(solution)/shard_map/all_gather | solution.py:171
  199.2 3.3 fusion.68
  208.2 3.7 reshape.276
  214.4 12.4 %all-gather.14.cloned.1.call-done = bf16[2048,768]{1,0:T(8,128)(2,1)} async-done(((bf16[512,768]{1,0:T(8,128)(2,1)}), bf16[2048,768]{1,0:T(8,128)(2,1)}) %all-gather.14.cloned.1.call-update) | async-done | bytes 3145744 | tf_op jit(solution)/shard_map/all_gather | solution.py:206
  226.8 5.1 fusion.71
  231.9 8.3 %convert_reduce_fusion = (f32[768]{0:T(1024)}, bf16[2048,768]{1,0:T(8,128)(2,1)S(1)}, bf16[2048,768]{1,0:T(8,128)(2,1)}) fusion(f32[2048,768]{1,0:T(8,128)S(1)} %fusion.71, f32[768]{0:T(1024)S(1)} %dynamic_slice.31, bf16[2048,768]{1,0:T(8,128)(2,1)S(1)} %copy-done.48, bf16[768,768]{0,1:T(8,128)(2,1)S(1)} %bitcast.206), kind=kOutput, calls=%fused_computation.64 | convolution fusion | flops 2455239936 | bytes 16914432 | tf_op jit(solution)/shard_map/dot_general | solution.py:47
  242.0 4.6 fusion.72
  247.1 6.6 %convolution_convert_fusion = bf16[2048,768]{1,0:T(8,128)(2,1)} fusion(bf16[2048,768]{1,0:T(8,128)(2,1)} %get-tuple-element.365, bf16[768,768]{0,1:T(8,128)(2,1)} %bitcast.205), kind=kOutput, calls=%fused_computation.67 | convolution fusion | flops 2417491968 | bytes 7471104 | tf_op jit(solution)/shard_map/dot_general | solution.py:209
  253.7 8.7 %fusion.74 = f32[768,768]{1,0:T(8,128)} fusion(bf16[2048,768]{1,0:T(8,128)(2,1)} %get-tuple-element.365, bf16[2048,768]{1,0:T(8,128)(2,1)} %all-gather.12.cloned.1.call-done), kind=kOutput, calls=%fused_computation.139 | convolution fusion | flops 2415919104 | bytes 8650752 | tf_op jit(solution)/shard_map/dot_general | solution.py:53
  262.4 4.1 fusion.73
  266.5 39.1 %reduce-scatter.7.cloned.1.call-done = f32[512,768]{1,0:T(8,128)} async-done(((f32[2048,768]{1,0:T(8,128)}), f32[512,768]{1,0:T(8,128)}) %reduce-scatter.7.cloned.1.call-update) | async-done | bytes 1572880 | tf_op jit(solution)/shard_map/reduce_scatter | solution.py:220
  312.0 3.5 reshape_reshape.13
  315.5 3.1 copy.82
  318.6 3.6 copy.83
  322.2 5.2 reshape.283
  327.3 13.3 %all-gather.16.cloned.1.call-done = bf16[2048,768]{1,0:T(8,128)(2,1)} async-done(((bf16[512,768]{1,0:T(8,128)(2,1)}), bf16[2048,768]{1,0:T(8,128)(2,1)}) %all-gather.16.cloned.1.call-update) | async-done | bytes 3145744 | tf_op jit(solution)/shard_map/all_gather | solution.py:232
  344.4 5.1 pad_maximum_fusion
  349.5 6.4 %reshape.284 = f32[1728,768]{1,0:T(8,128)} reshape(f32[8,165888]{1,0:T(8,128)} %pad_maximum_fusion) | data formatting | bytes 10616832 | tf_op jit(solution)/shard_map/reshape | solution.py:248
  356.5 3.1 convolution_convert_fusion.1
  360.4 137.5 %while.28 = (s32[]{:T(128)}, f32[2048,3,64]{0,2,1:T(8,128)}, f32[2048,3,64]{0,2,1:T(8,128)}, bf16[4,512,3,64]{1,3,2,0:T(8,128)(2,1)}, bf16[4,512,3,64]{1,3,2,0:T...) while((s32[]{:T(128)}, f32[2048,3,64]{0,2,1:T(8,128)}, ...), condition=%wide.region_13.14_spmd.clone, body=%wide.region_11.13_spmd.clone.sunk | while | flops 2064614400 | bytes 156684720 | solution.py:126
  366.4 4.9 fusion.144
  371.4 6.2 multiply_reduce_fusion.8
  377.5 6.3 %multiply_convert_fusion.3 = bf16[3,512,2048]{2,1,0:T(8,128)(2,1)} fusion(f32[3,512,2048]{2,1,0:T(8,128)S(1)} %get-tuple-element.504, f32[3,512,2048]{2,1,0:T(8,128)S(1)} %fusion.141, f32[3,512]{1,0:T(4,128)S(1)} %get-tuple-element.505, f32[3,512]{1,0:T(4,128)S(1)} %dynamic-slice_bitcast_fusion.2, pred[512,2048]{1,0:T(8,128)(4,1)} %copy-done.3), kind=kLoop, calls=%fused_computation.20.clone.1 | loop fusion | flops 18874368 | bytes 32518144 | tf_op jit(solution)/shard_map/while/body/eval_jaxpr/convert_element_type | solution.py:111
  383.8 5.8 fusion.145
  389.7 3.6 fusion.143
  396.1 3.0 fusion.141
  399.2 6.3 %fusion.144 = f32[2048,3,64]{0,2,1:T(8,128)} fusion(f32[3,512,2048]{2,1,0:T(8,128)S(1)} %fusion.141, f32[3,512]{1,0:T(4,128)S(1)} %dynamic-slice_bitcast_fusion.2, pred[512,2048]{1,0:T(8,128)(4,1)S(1)} %fusion.142, f32[2048,3,64]{0,2,1:T(8,128)} %get-tuple-element.548, pred[]{:T(512)S(6)} %compare.3, ...), kind=kOutput, calls=%fused_computation.32.clone.1 | convolution fusion | flops 416022528 | bytes 16982020 | tf_op jit(solution)/shard_map/while/body/eval_jaxpr/hqk,qhe->khe/dot_general | solution.py:104
  405.5 6.2 multiply_reduce_fusion.8
  411.7 6.3 %multiply_convert_fusion.3 = bf16[3,512,2048]{2,1,0:T(8,128)(2,1)} fusion(f32[3,512,2048]{2,1,0:T(8,128)S(1)} %get-tuple-element.504, f32[3,512,2048]{2,1,0:T(8,128)S(1)} %fusion.141, f32[3,512]{1,0:T(4,128)S(1)} %get-tuple-element.505, f32[3,512]{1,0:T(4,128)S(1)} %dynamic-slice_bitcast_fusion.2, pred[512,2048]{1,0:T(8,128)(4,1)} %copy-done.3), kind=kLoop, calls=%fused_computation.20.clone.1 | loop fusion | flops 18874368 | bytes 32518144 | tf_op jit(solution)/shard_map/while/body/eval_jaxpr/convert_element_type | solution.py:111
  418.0 5.9 fusion.145
  423.9 4.2 fusion.143
  434.0 6.4 %fusion.144 = f32[2048,3,64]{0,2,1:T(8,128)} fusion(f32[3,512,2048]{2,1,0:T(8,128)S(1)} %fusion.141, f32[3,512]{1,0:T(4,128)S(1)} %dynamic-slice_bitcast_fusion.2, pred[512,2048]{1,0:T(8,128)(4,1)S(1)} %fusion.142, f32[2048,3,64]{0,2,1:T(8,128)} %get-tuple-element.548, pred[]{:T(512)S(6)} %compare.3, ...), kind=kOutput, calls=%fused_computation.32.clone.1 | convolution fusion | flops 416022528 | bytes 16982020 | tf_op jit(solution)/shard_map/while/body/eval_jaxpr/hqk,qhe->khe/dot_general | solution.py:104
  440.4 6.2 multiply_reduce_fusion.8
  446.5 6.3 %multiply_convert_fusion.3 = bf16[3,512,2048]{2,1,0:T(8,128)(2,1)} fusion(f32[3,512,2048]{2,1,0:T(8,128)S(1)} %get-tuple-element.504, f32[3,512,2048]{2,1,0:T(8,128)S(1)} %fusion.141, f32[3,512]{1,0:T(4,128)S(1)} %get-tuple-element.505, f32[3,512]{1,0:T(4,128)S(1)} %dynamic-slice_bitcast_fusion.2, pred[512,2048]{1,0:T(8,128)(4,1)} %copy-done.3), kind=kLoop, calls=%fused_computation.20.clone.1 | loop fusion | flops 18874368 | bytes 32518144 | tf_op jit(solution)/shard_map/while/body/eval_jaxpr/convert_element_type | solution.py:111
  452.8 5.8 fusion.145
  458.7 4.2 fusion.143
  468.8 6.3 %fusion.144 = f32[2048,3,64]{0,2,1:T(8,128)} fusion(f32[3,512,2048]{2,1,0:T(8,128)S(1)} %fusion.141, f32[3,512]{1,0:T(4,128)S(1)} %dynamic-slice_bitcast_fusion.2, pred[512,2048]{1,0:T(8,128)(4,1)S(1)} %fusion.142, f32[2048,3,64]{0,2,1:T(8,128)} %get-tuple-element.548, pred[]{:T(512)S(6)} %compare.3, ...), kind=kOutput, calls=%fused_computation.32.clone.1 | convolution fusion | flops 416022528 | bytes 16982020 | tf_op jit(solution)/shard_map/while/body/eval_jaxpr/hqk,qhe->khe/dot_general | solution.py:104
  475.1 6.2 multiply_reduce_fusion.8
  481.3 6.3 %multiply_convert_fusion.3 = bf16[3,512,2048]{2,1,0:T(8,128)(2,1)} fusion(f32[3,512,2048]{2,1,0:T(8,128)S(1)} %get-tuple-element.504, f32[3,512,2048]{2,1,0:T(8,128)S(1)} %fusion.141, f32[3,512]{1,0:T(4,128)S(1)} %get-tuple-element.505, f32[3,512]{1,0:T(4,128)S(1)} %dynamic-slice_bitcast_fusion.2, pred[512,2048]{1,0:T(8,128)(4,1)} %copy-done.3), kind=kLoop, calls=%fused_computation.20.clone.1 | loop fusion | flops 18874368 | bytes 32518144 | tf_op jit(solution)/shard_map/while/body/eval_jaxpr/convert_element_type | solution.py:111
  487.6 5.9 fusion.145
  493.5 4.2 fusion.143
  509.3 5.9 fusion.56
  524.7 3.8 all-to-all-start.1
  535.7 21.2 %all-to-all-done.1 = bf16[4,512,3,192]{1,3,2,0:T(8,128)(2,1)S(1)} async-done(((bf16[4,512,3,192]{1,3,2,0:T(8,128)(2,1)}), bf16[4,512,3,192]{1,3,2,0:T(8,128)(2,1)S(1)}, u32[]{:S(2)}, u32[]{:S(2)}) %all-to-all-start.1) | async-done | bytes 2359328 | tf_op jit(solution)/shard_map/all_to_all | solution.py:18
  558.3 3.3 copy.84
  561.7 5.4 fusion.54
  568.6 41.7 %all-reduce = (f32[768]{0:T(1024)}, f32[768]{0:T(1024)}, f32[2,768]{1,0:T(2,128)}, f32[768]{0:T(1024)}, f32[768]{0:T(1024)}, /*index=5*/f32[768]{0:T(1024)}, f32[3072]{0:T(1024)}, f32[768]{0:T(1024)}, f32[5,768]{1,0:T(8,128)}) all-reduce(f32[768]{0:T(1024)S(1)} %get-tuple-element.298, ...), channel_id=1, replica_groups=mesh['fsdp'=8,'tp'=4] {'fsdp','tp'}, use_global_device_ids=true, to_apply=%region_20.21 | all-reduce | flops 13056 | bytes 104448 | tf_op jit(solution)/shard_map/psum | solution.py:298
  (307 shorter events, 113.4 us)
Async XLA Ops:
  7.2 4.0 copy-start.41
  7.2 4.0 copy-start.44
  7.2 45.7 %all-gather.10.cloned.1.call-start = ((), (), s32[]{:S(2)}) async-start(), calls=%async_computation.6 | async-start | bytes 3932160 | tf_op jit(solution)/shard_map/all_gather | solution.py:170
  11.2 41.0 %copy-start.35 = (f32[512]{0:T(512)}, f32[512]{0:T(512)S(1)}, u32[]{:S(2)}) copy-start(f32[512]{0:T(512)S(1)} %add_rsqrt_fusion.1) | copy-start | bytes 6148
  12.4 144.7 %all-gather.20.cloned.1.call-start = ((), (), s32[]{:S(2)}) async-start(), calls=%async_computation.14 | async-start | bytes 2654208 | tf_op jit(solution)/shard_map/all_gather | solution.py:183
  52.9 108.6 %all-gather.12.cloned.1.call-start = ((), (), s32[]{:S(2)}) async-start(), calls=%async_computation.7 | async-start | bytes 3932160 | tf_op jit(solution)/shard_map/all_gather | solution.py:185
  53.7 136.4 %all-gather.22.cloned.1.call-start = ((), (), s32[]{:S(2)}) async-start(), calls=%async_computation.15 | async-start | bytes 1622016 | tf_op jit(solution)/shard_map/all_gather | solution.py:171
  56.2 4.2 copy-start.23
  156.3 5.2 copy-start.14
  157.1 4.4 copy-start.16
  162.5 32.2 %all-to-all-start = ((bf16[4,512,192]{1,2,0:T(8,128)(2,1)}), bf16[4,512,192]{1,2,0:T(8,128)(2,1)}, u32[]{:S(2)}, u32[]{:S(2)}) async-start(bf16[4,512,192]{1,2,0:T(8,128)(2,1)} %bitcast.146), calls=%async_computation | async-start | bytes 1572864 | tf_op jit(solution)/shard_map/all_to_all | solution.py:200
  166.7 60.1 %all-gather.14.cloned.1.call-start = ((), (), s32[]{:S(2)}) async-start(), calls=%async_computation.8 | async-start | bytes 3932160 | tf_op jit(solution)/shard_map/all_gather | solution.py:206
  190.1 4.6 copy-start.50
  197.6 110.9 %copy-start.8 = (f32[512,768]{1,0:T(8,128)}, f32[512,768]{1,0:T(8,128)S(1)}, u32[]{:S(2)}) copy-start(f32[512,768]{1,0:T(8,128)S(1)} %get-tuple-element.378) | copy-start | bytes 4718596
  199.2 106.4 %reduce-scatter.7.cloned.1.call-start = ((), (), s32[]{:S(2)}) async-start(), calls=%async_computation.9 | async-start | bytes 7864320 | tf_op jit(solution)/shard_map/reduce_scatter | solution.py:220
  226.8 5.1 copy-start.28
  226.8 5.1 copy-start.48
  231.9 10.1 %copy-start.27 = (bf16[768,768]{1,0:T(8,128)(2,1)S(1)}, bf16[768,768]{1,0:T(8,128)(2,1)}, u32[]{:S(2)}) copy-start(bf16[768,768]{1,0:T(8,128)(2,1)} %reshape_reshape.11) | copy-start | bytes 3538948
  246.6 94.0 %all-gather.16.cloned.1.call-start = ((), (), s32[]{:S(2)}) async-start(), calls=%async_computation.10 | async-start | bytes 3932160 | tf_op jit(solution)/shard_map/all_gather | solution.py:232
  253.7 8.7 %copy-start.49 = (bf16[2048,768]{1,0:T(8,128)(2,1)S(1)}, bf16[2048,768]{1,0:T(8,128)(2,1)}, u32[]{:S(2)}) copy-start(bf16[2048,768]{1,0:T(8,128)(2,1)} %all-gather.14.cloned.1.call-done) | copy-start | bytes 9437188
  253.7 8.7 %copy-start.52 = (bf16[2048,768]{1,0:T(8,128)(2,1)S(1)}, bf16[2048,768]{1,0:T(8,128)(2,1)}, u32[]{:S(2)}) copy-start(bf16[2048,768]{1,0:T(8,128)(2,1)} %copy-done.51) | copy-start | bytes 9437188
  312.0 192.3 %reduce-scatter.9.cloned.1.call-start = ((), (), s32[]{:S(2)}) async-start(), calls=%async_computation.11 | async-start | bytes 3932160 | tf_op jit(solution)/shard_map/reduce_scatter | solution.py:236
  322.2 18.5 %copy-start.17 = (bf16[24,8,4,512]{3,1,2,0:T(8,128)(2,1)S(1)}, bf16[24,8,4,512]{3,1,2,0:T(8,128)(2,1)}, u32[]{:S(2)}) copy-start(bf16[24,8,4,512]{3,1,2,0:T(8,128)(2,1)} %copy-done.16) | copy-start | bytes 2359300
  343.4 163.3 %reduce-scatter.11.cloned.1.call-start = ((), (), s32[]{:S(2)}) async-start(), calls=%async_computation.12 | async-start | bytes 5971968 | tf_op jit(solution)/shard_map/reduce_scatter | solution.py:247
  355.9 205.8 %all-gather.18.cloned.1.call-start = ((), (), s32[]{:S(2)}) async-start(), calls=%async_computation.13 | async-start | bytes 4423680 | tf_op jit(solution)/shard_map/all_gather | solution.py:184
  356.5 253.8 %reduce-scatter.13.cloned.1.call-start = ((), (), s32[]{:S(2)}) async-start(), calls=%async_computation.16 | async-start | bytes 2211840
  360.5 5.8 copy-start.4
  360.5 5.8 copy-start.6
  360.6 5.8 copy-start.21
  383.8 5.8 copy-start.2
  389.7 3.6 copy-start.5
  389.7 3.6 copy-start.7
  389.7 3.6 copy-start.22
  393.3 5.9 copy-start.4
  393.3 5.9 copy-start.6
  393.3 5.9 copy-start.21
  418.0 5.9 copy-start.2
  423.9 4.2 copy-start.5
  423.9 4.2 copy-start.7
  423.9 4.2 copy-start.22
  428.1 5.9 copy-start.4
  428.1 5.9 copy-start.6
  428.1 5.9 copy-start.21
  452.8 5.8 copy-start.2
  458.7 4.2 copy-start.5
  458.7 4.2 copy-start.7
  458.7 4.2 copy-start.22
  462.9 5.9 copy-start.4
  462.9 5.9 copy-start.6
  462.9 5.9 copy-start.21
  487.6 5.9 copy-start.2
  493.5 4.2 copy-start.5
  493.5 4.2 copy-start.7
  493.5 4.2 copy-start.22
  524.7 3.8 copy-start.47
  524.7 4.1 copy-start.26
  524.7 32.2 %all-to-all-start.1 = ((bf16[4,512,3,192]{1,3,2,0:T(8,128)(2,1)}), bf16[4,512,3,192]{1,3,2,0:T(8,128)(2,1)S(1)}, u32[]{:S(2)}, u32[]{:S(2)}) async-start(bf16[4,512,3,192]{1,3,2,0:T(8,128)(2,1)} %pad_maximum_fusion.2), calls=%async_computation.4 | async-start | bytes 4718592 | tf_op jit(solution)/shard_map/all_to_all | solution.py:18
  558.3 3.4 copy-start.11
  558.3 3.4 copy-start.34
  558.3 3.4 copy-start.36
  558.3 3.4 copy-start.42
  561.7 5.5 copy-start.13
  567.2 44.9 %copy-start.1 = (f32[5,768]{1,0:T(8,128)S(1)}, f32[5,768]{1,0:T(8,128)}, u32[]{:S(2)}) copy-start(f32[5,768]{1,0:T(8,128)} %param.37) | copy-start | bytes 46084
  567.9 44.3 %copy-start.18 = (f32[512,768]{1,0:T(8,128)}, f32[512,768]{1,0:T(8,128)S(1)}, u32[]{:S(2)}) copy-start(f32[512,768]{1,0:T(8,128)S(1)} %multiply_add_fusion) | copy-start | bytes 4718596
  (26 other events, 54.5 us)
Sparse Core Ops, SparseCore 0:
  12.5 31.2 all-gather.9
  53.0 50.7 all-gather.19
  105.4 27.0 all-gather.11
  135.1 54.8 all-gather.21
  199.3 27.4 all-gather.13
  246.7 58.8 reduce-scatter.6
  312.1 28.4 all-gather.15
  343.5 37.8 reduce-scatter.8
  385.0 104.4 reduce-scatter.10
  490.9 30.3 all-gather.17
  524.8 67.6 reduce-scatter.12
